TPU v7x, 32 devices: a whole 2x2x4 slice. The times are simulated.
32 devices in a mesh: det: 4 (over y, x), tm: 8 (over z, core).
Axes of the slice: x: 2, y: 2, z: 4, core: 2. Of those that a mesh axis runs over, the one named last changes fastest.
Arguments:
- sol_map: float32 [3, 49152], P(None, ('det', 'tm')), may hold values from -6 to 6
- resid_map: float32 [3, 49152], P(None, ('det', 'tm')), may hold values from -6 to 6
- direction: float32 [3, 49152], P(None, ('det', 'tm')), may hold values from -6 to 6
- precond: float32 [3, 49152], P(None, ('det', 'tm')), may hold values from 0.1 to 1
- pixels: int32 [128, 65536], P('det', 'tm'), may hold values from 0 to 49151
- angle_index: int32 [128, 65536], P('det', 'tm'), may hold values from 0 to 127
- angles: float32 [128], replicated, may hold values from -3.140625 to 3.140625
- flag_mask: int32 [128, 65536], P('det', 'tm'), may hold values 0 or 1
- inv_noise: float32 [128, 32769], P(('det', 'tm')), may hold values from 0.05 to 1
Outputs:
- new_sol: float32 [3, 49152], P(None, ('det', 'tm'))
- new_resid: float32 [3, 49152], P(None, ('det', 'tm'))
- new_dir: float32 [3, 49152], P(None, ('det', 'tm'))
- new_norm: float32 [], replicated
All inputs are finite; a program needn't handle non-finite values. No bound on the sum of `flag_mask` on one device may be relied on, other than what follows from the above.
Results may differ from a plain program's by a relative error of at most 0.0001.
Values sent between devices are 32-bit elements; how exact they have to be, the bound alone decides.
A program may use at most 320 MiB of HBM per device.

v0:
```python
import math

import jax
import jax.numpy as jnp
from jax import lax
from jax.sharding import PartitionSpec as P


def product(form, left, right):
    return jnp.einsum(form, left, right, precision=lax.Precision.HIGHEST)


def trig_lookup(angle_index, angles):
    levels = angles.shape[0]
    tables = jnp.stack([jnp.cos(2.0 * angles), jnp.sin(2.0 * angles)])
    level_ids = jnp.arange(levels, dtype=jnp.int32)
    match = angle_index[None, :, :, None] == level_ids
    picked = jnp.sum(jnp.where(match, tables[:, None, None, :], 0.0), axis=3)
    return (picked[0], picked[1])


def noise_weight(series, filt):
    n_series, total_len = series.shape
    side_len = math.isqrt(total_len)
    indices = jnp.arange(side_len, dtype=jnp.int32)
    products = indices[:, None] * indices[None, :]
    angle_tab = 2.0 * math.pi / side_len * (products % side_len).astype(jnp.float32)
    f_real = jnp.cos(angle_tab)
    f_imag = -jnp.sin(angle_tab)
    twist = products.astype(jnp.float32) * (2.0 * math.pi / total_len)
    w_real = jnp.cos(twist)
    w_imag = -jnp.sin(twist)
    matrix_form = series.reshape(n_series, side_len, side_len)
    y_real = product("kt,dtu->dku", f_real, matrix_form)
    y_imag = product("kt,dtu->dku", f_imag, matrix_form)
    y_real, y_imag = (y_real * w_real - y_imag * w_imag, y_real * w_imag + y_imag * w_real)
    z_real = product("dku,uv->dvk", y_real, f_real) - product("dku,uv->dvk", y_imag, f_imag)
    z_imag = product("dku,uv->dvk", y_real, f_imag) + product("dku,uv->dvk", y_imag, f_real)
    half_len = filt.shape[1]
    mirror = jnp.flip(filt[:, 1 : half_len - 1], axis=1)
    weight = jnp.concatenate([filt, mirror], 1).reshape(n_series, side_len, side_len)
    z_real = z_real * weight
    z_imag = z_imag * weight
    v_real = product("dvk,vu->dku", z_real, f_real) + product("dvk,vu->dku", z_imag, f_imag)
    v_imag = product("dvk,vu->dku", z_imag, f_real) - product("dvk,vu->dku", z_real, f_imag)
    v_real, v_imag = (v_real * w_real + v_imag * w_imag, v_imag * w_real - v_real * w_imag)
    result = product("tk,dku->dtu", f_real, v_real) + product("tk,dku->dtu", f_imag, v_imag)
    return (result / total_len).reshape(n_series, total_len)


def body(sol_map, resid_map, direction, precond, pixels, angle_index, angles, flag_mask, inv_noise):
    full_dir = lax.all_gather(direction, ("det", "tm"), axis=1, tiled=True)
    det_rows, samples = pixels.shape
    n_pixels = full_dir.shape[1]
    share_len = direction.shape[1]
    cos_two, sin_two = trig_lookup(angle_index, angles)
    usable = flag_mask.astype(jnp.float32)
    flat_pix = pixels.reshape(-1)
    stokes = jnp.take(full_dir, flat_pix, axis=1).reshape(3, det_rows, samples)
    signal = usable * (stokes[0] + stokes[1] * cos_two + stokes[2] * sin_two)
    by_detector = lax.all_to_all(signal, "tm", split_axis=0, concat_axis=1, tiled=True)
    filtered = noise_weight(by_detector, inv_noise)
    returned = lax.all_to_all(filtered, "tm", split_axis=1, concat_axis=0, tiled=True)
    weighted = usable * returned
    contrib = jnp.stack([weighted, weighted * cos_two, weighted * sin_two]).reshape(3, -1)
    partial_map = jnp.zeros((3, n_pixels), jnp.float32).at[:, flat_pix].add(contrib)
    whole = lax.psum(partial_map, ("det", "tm"))
    offset = lax.axis_index(("det", "tm")) * share_len
    image = lax.dynamic_slice_in_dim(whole, offset, share_len, 1)
    scaled_resid = precond * resid_map
    norm_old, curvature, cross_term, image_norm = lax.psum(
        (
            jnp.sum(scaled_resid * resid_map),
            jnp.sum(direction * image),
            jnp.sum(image * scaled_resid),
            jnp.sum(image * precond * image),
        ),
        ("det", "tm"),
    )
    step_size = norm_old / curvature
    new_resid = resid_map - step_size * image
    new_norm = norm_old - 2.0 * step_size * cross_term + step_size * step_size * image_norm
    new_sol = sol_map + step_size * direction
    new_dir = precond * new_resid + new_norm / norm_old * direction
    return (new_sol, new_resid, new_dir, new_norm)


def solution(mesh):
    in_specs = (
        P(None, ("det", "tm")),
        P(None, ("det", "tm")),
        P(None, ("det", "tm")),
        P(None, ("det", "tm")),
        P("det", "tm"),
        P("det", "tm"),
        P(),
        P("det", "tm"),
        P(("det", "tm"), None),
    )
    out_specs = (P(None, ("det", "tm")), P(None, ("det", "tm")), P(None, ("det", "tm")), P())
    return jax.shard_map(body, mesh=mesh, in_specs=in_specs, out_specs=out_specs, check_vma=False)
```

profile of v0, /device:TPU:0, one launch (start us, length us, event | category | flops | bytes accessed | tf_op | source)
XLA Modules:
  0.0 3372.7 jit_solution(5624651137445883188)
XLA Ops:
  7.2 2.4 copy.220
  9.6 1.1 compare_select_fusion
  10.7 0.0 copy-start.2
  10.7 1.1 copy-done.2
  11.8 0.1 broadcast_clamp_fusion
  11.9 1.0 copy.172
  12.9 275.5 %all_gather.3 = f32[3,49152]{0,1:T(8,128)} all-gather(f32[3,1536]{0,1:T(8,128)S(1)} %copy.172), channel_id=1, replica_groups=mesh['det'=4,'tm'=8] {'det','tm'}, dimensions={1}, use_global_device_ids=true | all-gather | bytes 608256 | tf_op jit(solution)/shard_map/all_gather | solution.py:52
  288.5 0.2 copy.221
  288.7 0.3 compare_and_fusion
  289.0 868.1 %gather_fusion = f32[262144,3]{1,0:T(8,128)} fusion(f32[3,49152]{0,1:T(8,128)} %all_gather.3, s32[262144]{0:T(1024)S(1)} %broadcast_clamp_fusion), kind=kCustom, calls=%fused_computation | custom fusion | bytes 7340032 | tf_op jit(solution)/shard_map/jit(_take)/gather | solution.py:59
  1157.1 132.7 %select_bitcast_fusion = f32[3,262144]{0,1:T(8,128)} fusion(f32[262144,3]{1,0:T(8,128)} %gather_fusion, pred[262144]{0:T(1024)(128)(4,1)S(1)} %compare_and_fusion), kind=kLoop, calls=%fused_computation.6 | loop fusion | flops 786432 | bytes 6553600 | tf_op jit(solution)/shard_map/jit(_take)/select_n | solution.py:59
  1289.8 184.4 %slice_reduce_fusion.1 = (f32[262144]{0:T(1024)S(1)}, f32[262144]{0:T(1024)S(1)}, f32[262144]{0:T(1024)S(1)}) fusion(f32[3,262144]{0,1:T(8,128)} %select_bitcast_fusion), kind=kLoop, calls=%fused_computation.4 | loop fusion | bytes 6291456 | tf_op jit(solution)/shard_map/slice | solution.py:60
  1474.2 1.2 squeeze.15
  1475.4 1.2 squeeze.16
  1476.6 1.2 squeeze.18
  1477.8 0.0 copy-start
  1477.8 42.7 %iota_compare_fusion = pred[32,8192,128]{2,1,0:T(8,128)(4,1)} fusion(s32[32,8192]{1,0:T(8,128)} %param.14), kind=kLoop, calls=%fused_computation.7 | loop fusion | flops 33554432 | bytes 34603008 | tf_op jit(solution)/shard_map/eq | solution.py:17
  1520.5 77.1 %select_reduce_fusion = f32[2,32,8192]{2,1,0:T(8,128)S(1)} fusion(f32[2,128]{1,0:T(2,128)S(1)} %pad_maximum_fusion.1, pred[32,8192,128]{2,1,0:T(8,128)(4,1)} %iota_compare_fusion), kind=kLoop, calls=%fused_computation.2 | loop fusion | flops 133693440 | bytes 35652608 | tf_op jit(solution)/shard_map/reduce_sum | solution.py:18
  1597.6 0.0 copy-done
  1597.6 3.1 add_multiply_fusion
  1600.7 2.5 all_to_all.26
  1603.3 4.2 all-to-all-start
  1607.5 0.0 all-reduce.3.cloned.1.call-start
  1607.6 1.4 slice.26
  1608.9 22.6 reverse
  1631.5 0.3 slice.47
  1631.9 2.4 pad_maximum_fusion
  1634.3 0.9 fusion.38
  1635.1 0.1 copy.175
  1635.3 0.9 sine_negate_fusion
  1636.2 0.1 copy.177
  1636.3 0.0 all-to-all-done
  1636.3 2.8 copy.173
  1639.1 2.4 reshape.113
  1641.5 3.8 convolution_bitcast_fusion
  1645.4 3.8 convolution_bitcast_fusion.1
  1649.3 2.1 fusion.36
  1651.4 2.3 fusion.22
  1653.6 3.5 fusion.7
  1657.2 2.0 fusion.33
  1659.2 3.5 fusion.5
  1662.7 2.0 fusion.31
  1664.8 2.3 convolution_add_fusion.1
  1667.1 2.1 convolution_subtract_fusion
  1669.2 2.0 fusion.11
  1671.2 3.1 fusion.3
  1674.3 1.6 copy.194
  1675.8 1.2 all_to_all.29
  1677.0 1.9 copy.195
  1678.9 31.7 all_to_all.35
  1710.6 1.6 all_to_all.32
  1712.2 1.5 multiply_bitcast_fusion.1
  1713.7 1.1 copy.223
  1714.8 1.1 copy.224
  1715.9 1.1 copy.225
  1716.9 4.2 maximum_bitcast_fusion
  1721.2 58.5 %copy.196 = f32[262144,3]{1,0:T(8,128)} copy(f32[262144,3]{0,1:T(4,128)} %maximum_bitcast_fusion) | data formatting | bytes 6291456 | tf_op jit(solution)/shard_map/stack | solution.py:65
  1779.7 1396.5 %scatter_custom_fusion = f32[3,49152]{0,1:T(8,128)} fusion(s32[262144]{0:T(1024)} %bitcast.105, f32[262144,3]{1,0:T(8,128)} %copy.196, f32[]{:T(128)} %constant.18.clone.1), kind=kCustom, calls=%fused_computation.8 | custom fusion | flops 786432 | bytes 590336 | tf_op jit(solution)/shard_map/scatter-add | solution.py:66
  3176.2 14.1 copy.197
  3190.4 0.0 all-reduce.3.cloned.1.call-update
  3190.4 127.5 %all-reduce.3.cloned.1.call-done = f32[3,49152]{1,0:T(4,128)} async-done(((f32[3,49152]{1,0:T(4,128)}), f32[3,49152]{1,0:T(4,128)}) %all-reduce.3.cloned.1.call-update) | async-done | bytes 589840 | tf_op jit(solution)/shard_map/psum | solution.py:67
  3317.9 1.4 fusion.49
  3319.3 39.6 %all-reduce = (f32[]{:T(128)}, f32[]{:T(128)}, f32[]{:T(128)}, f32[]{:T(128)}) all-reduce(f32[]{:T(128)} %get-tuple-element.26, f32[]{:T(128)} %get-tuple-element.25, f32[]{:T(128)} %get-tuple-element.24, f32[]{:T(128)} %get-tuple-element.23), channel_id=1, replica_groups=mesh['det'=4,'tm'=8] {'det','tm'}, use_global_device_ids=true, to_apply=%region_1.2 | all-reduce | flops 4 | bytes 32 | tf_op jit(solution)/shard_map/psum | solution.py:71
  3362.9 1.4 multiply_add_fusion.3
  (14 shorter events, 0.1 us)
Async XLA Ops:
  7.2 281.3 %copy-start.1 = (s32[32,8192]{1,0:T(8,128)S(1)}, s32[32,8192]{1,0:T(8,128)}, u32[]{:S(2)}) copy-start(s32[32,8192]{1,0:T(8,128)} %param.13) | copy-start | bytes 3145732
  10.7 1.1 copy-start.2
  1289.8 187.9 %copy-start.7 = (f32[128]{0:T(128)S(1)}, f32[128]{0:T(128)}, u32[]{:S(2)}) copy-start(f32[128]{0:T(128)} %param.15) | copy-start | bytes 1540
  1477.8 119.8 %copy-start = (s32[32,8192]{1,0:T(8,128)S(1)}, s32[32,8192]{1,0:T(8,128)}, u32[]{:S(2)}) copy-start(s32[32,8192]{1,0:T(8,128)} %param.16) | copy-start | bytes 3145732
  1603.3 33.0 all-to-all-start
  1607.5 1710.4 %all-reduce.3.cloned.1.call-start = ((), (), s32[]{:S(2)}) async-start(), calls=%async_computation.2 | async-start | bytes 1572864 | tf_op jit(solution)/shard_map/psum | solution.py:67
  1779.7 1538.2 %copy-start.3 = (f32[3,1536]{1,0:T(4,128)S(1)}, f32[3,1536]{1,0:T(4,128)}, u32[]{:S(2)}) copy-start(f32[3,1536]{1,0:T(4,128)} %param.11) | copy-start | bytes 55300
  1779.7 1538.2 %copy-start.4 = (f32[3,1536]{1,0:T(4,128)S(1)}, f32[3,1536]{1,0:T(4,128)}, u32[]{:S(2)}) copy-start(f32[3,1536]{1,0:T(4,128)} %param.12) | copy-start | bytes 55300
  1779.7 1538.2 %copy-start.5 = (f32[3,1536]{1,0:T(4,128)S(1)}, f32[3,1536]{1,0:T(4,128)}, u32[]{:S(2)}) copy-start(f32[3,1536]{1,0:T(4,128)} %param.10) | copy-start | bytes 55300
  1779.7 1583.2 %copy-start.6 = (f32[3,1536]{1,0:T(4,128)S(1)}, f32[3,1536]{1,0:T(4,128)}, u32[]{:S(2)}) copy-start(f32[3,1536]{1,0:T(4,128)} %param.9) | copy-start | bytes 55300
Sparse Core Ops, SparseCore 0:
  3190.5 127.3 all-reduce.2
where the time goes:
time: 3380 us; the launch traced here: 3370 us
  other arithmetic  1670 us (49%)
  local copies, waits for them, and re-layouts  1180 us (35%)
  blocking collectives  347 us (10%)
  waiting for transfers between devices  128 us (4%)
    scatter-add x1, other arithmetic, body(): jnp.zeros((3, n_pixels), jnp.float32).at[:, flat_pix].add(contrib)  1400 us
    gather x1, local copies, waits for them, and re-layouts, body(): stokes = jnp.take(full_dir, flat_pix, axis=1).reshape(3, det_rows, samples)  868 us
    all_gather x1, blocking collectives, body(): full_dir = lax.all_gather(direction, ('det', 'tm'), axis=1, tiled=True)  276 us
    slice x1, local copies, waits for them, and re-layouts, body(): signal = usable * (stokes[0] + stokes[1] * cos_two + stokes[2] * sin_two)  184 us
    select_n x1, other arithmetic, body(): stokes = jnp.take(full_dir, flat_pix, axis=1).reshape(3, det_rows, samples)  133 us
    psum x1, waiting for transfers between devices, body(): whole = lax.psum(partial_map, ('det', 'tm'))  128 us
    reduce_sum x1, other arithmetic, trig_lookup(): picked = jnp.sum(jnp.where(match, tables[:, None, None, :], 0.0), axis=3)  77.1 us
  transfers between devices with their start and end apart: 2, of which 1 were waited for; matrix products, arithmetic and copies ran while one was open for 1% of the time, Pallas kernels for 0%

commit v1 on v0

v1 whole, which is shorter than its diff:
```python
import functools
import math

import jax
import jax.numpy as jnp
from jax import lax
from jax.experimental import pallas as pl
from jax.experimental.pallas import tpu as pltpu
from jax.sharding import PartitionSpec as P

LOW = 256
ROWS = 8
PACK = 16
LANES = 128
WIDTH = 512


def product(form, left, right, precision=lax.Precision.HIGH):
    return jnp.einsum(form, left, right, precision=precision)


def split_two(values):
    upper = values.astype(jnp.bfloat16)
    lower = (values - upper.astype(jnp.float32)).astype(jnp.bfloat16)
    return upper, lower


def lookup(table_row, index):
    rows, width = index.shape
    table = jnp.broadcast_to(table_row, (rows, LANES))
    parts = []
    for start in range(0, width, LANES):
        parts.append(jnp.take_along_axis(table, index[:, start : start + LANES], axis=1, mode="promise_in_bounds"))
    return jnp.concatenate(parts, axis=1)


def one_hot(row, size):
    ids = lax.broadcasted_iota(jnp.int32, (size, row.shape[1]), 0)
    return jnp.where(ids == row, 1.0, 0.0).astype(jnp.bfloat16)


def read_kernel(trig_ref, table_ref, pix_ref, ang_ref, flag_ref, out_ref, split_ref, *, high):
    @pl.when(pl.program_id(0) * pl.num_programs(1) + pl.program_id(1) == 0)
    def _():
        upper, lower = split_two(table_ref[...])
        split_ref[:, :LOW] = upper
        split_ref[:, LOW:] = lower

    cos_two = lookup(trig_ref[0:1, :], ang_ref[...])
    sin_two = lookup(trig_ref[1:2, :], ang_ref[...])
    usable = flag_ref[...].astype(jnp.float32)
    pix = pix_ref[...]
    pix_low = pix & (LOW - 1)
    pix_high = pix // LOW if LOW & (LOW - 1) else pix >> (LOW.bit_length() - 1)
    width = pix.shape[1]
    ids = lax.broadcasted_iota(jnp.int32, (high, width), 0)
    for row in range(ROWS):
        hot = one_hot(pix_low[row : row + 1], LOW)
        got = jnp.dot(split_ref[...], jnp.concatenate([hot, hot], axis=0), preferred_element_type=jnp.float32)
        mixed = got[:high] + got[high : 2 * high] * cos_two[row : row + 1] + got[2 * high :] * sin_two[row : row + 1]
        picked = jnp.sum(jnp.where(ids == pix_high[row : row + 1], mixed, 0.0), axis=0, keepdims=True)
        out_ref[row : row + 1, :] = picked * usable[row : row + 1]


def bin_kernel(trig_ref, pix_ref, ang_ref, flag_ref, val_ref, out_ref, *, high):
    step = pl.program_id(0) * pl.num_programs(1) + pl.program_id(1)

    @pl.when(step == 0)
    def _():
        out_ref[...] = jnp.zeros_like(out_ref)

    cos_two = lookup(trig_ref[0:1, :], ang_ref[...])
    sin_two = lookup(trig_ref[1:2, :], ang_ref[...])
    weighted = flag_ref[...].astype(jnp.float32) * val_ref[...]
    pieces = []
    for stokes in (weighted, weighted * cos_two, weighted * sin_two):
        upper = stokes.astype(jnp.bfloat16).astype(jnp.float32)
        pieces.append((upper, stokes - upper))
    pix = pix_ref[...]
    pix_low = pix & (LOW - 1)
    pix_high = pix >> (LOW.bit_length() - 1)
    total = None
    for row in range(ROWS):
        hot_low = one_hot(pix_low[row : row + 1], LOW)
        hot_high = one_hot(pix_high[row : row + 1], high)
        hot_high = hot_high.reshape(high // PACK, PACK, hot_high.shape[1])
        stack = []
        for part in range(2):
            for stokes in range(3):
                value = pieces[stokes][part][row : row + 1]
                value = jnp.broadcast_to(value, (PACK, value.shape[1])).astype(jnp.bfloat16)
                stack.append((hot_high * value[None]).reshape(high, value.shape[1]))
        left = jnp.concatenate(stack, axis=0)
        got = lax.dot_general(left, hot_low, (((1,), (1,)), ((), ())), preferred_element_type=jnp.float32)
        total = got if total is None else total + got
    out_ref[...] += total


def read_map(trig, table, pixels, angle_index, flag_mask):
    n_det, n_samp = pixels.shape
    high = table.shape[0] // 3
    block = pl.BlockSpec((ROWS, WIDTH), lambda i, j: (i, j))
    fixed = lambda shape: pl.BlockSpec(shape, lambda i, j: (0, 0))
    return pl.pallas_call(
        functools.partial(read_kernel, high=high),
        out_shape=jax.ShapeDtypeStruct((n_det, n_samp), jnp.float32),
        grid=(n_det // ROWS, n_samp // WIDTH),
        in_specs=[fixed(trig.shape), fixed(table.shape), block, block, block],
        out_specs=block,
        scratch_shapes=[pltpu.VMEM((3 * high, 2 * LOW), jnp.bfloat16)],
        compiler_params=pltpu.CompilerParams(dimension_semantics=("arbitrary", "arbitrary")),
        name="read_map",
    )(trig, table, pixels, angle_index, flag_mask)


def bin_map(trig, pixels, angle_index, flag_mask, values, high):
    n_det, n_samp = pixels.shape
    block = pl.BlockSpec((ROWS, WIDTH), lambda i, j: (i, j))
    fixed = lambda shape: pl.BlockSpec(shape, lambda i, j: (0, 0))
    pieces = pl.pallas_call(
        functools.partial(bin_kernel, high=high),
        out_shape=jax.ShapeDtypeStruct((6 * high, LOW), jnp.float32),
        grid=(n_det // ROWS, n_samp // WIDTH),
        in_specs=[fixed(trig.shape), block, block, block, block],
        out_specs=fixed((6 * high, LOW)),
        compiler_params=pltpu.CompilerParams(dimension_semantics=("arbitrary", "arbitrary")),
        name="bin_map",
    )(trig, pixels, angle_index, flag_mask, values)
    return pieces[: 3 * high] + pieces[3 * high :]


def mirrored(filt, side_len):
    n_series, half_len = filt.shape
    rows = (half_len - 1) // side_len
    lower = filt[:, : half_len - 1].reshape(n_series, rows, side_len)
    shifted = filt[:, 1:].reshape(n_series, rows, side_len)
    swap_col = jnp.flip(jnp.eye(side_len, dtype=jnp.float32), 0)
    swap_row = jnp.flip(jnp.eye(rows, dtype=jnp.float32), 0)
    exact = lax.Precision.HIGHEST
    upper = product("wv,dvk->dwk", swap_row, product("dvk,kl->dvl", shifted, swap_col, exact), exact)
    return jnp.concatenate([lower, upper], axis=1)


def noise_weight(series, filt):
    n_series, total_len = series.shape
    side_len = math.isqrt(total_len)
    indices = jnp.arange(side_len, dtype=jnp.int32)
    products = indices[:, None] * indices[None, :]
    angle_tab = 2.0 * math.pi / side_len * (products % side_len).astype(jnp.float32)
    f_real = jnp.cos(angle_tab)
    f_imag = -jnp.sin(angle_tab)
    twist = products.astype(jnp.float32) * (2.0 * math.pi / total_len)
    w_real = jnp.cos(twist)
    w_imag = -jnp.sin(twist)
    matrix_form = series.reshape(n_series, side_len, side_len)
    y_real = product("kt,dtu->dku", f_real, matrix_form)
    y_imag = product("kt,dtu->dku", f_imag, matrix_form)
    y_real, y_imag = (y_real * w_real - y_imag * w_imag, y_real * w_imag + y_imag * w_real)
    z_real = product("dku,uv->dvk", y_real, f_real) - product("dku,uv->dvk", y_imag, f_imag)
    z_imag = product("dku,uv->dvk", y_real, f_imag) + product("dku,uv->dvk", y_imag, f_real)
    weight = mirrored(filt, side_len)
    z_real = z_real * weight
    z_imag = z_imag * weight
    v_real = product("dvk,vu->dku", z_real, f_real) + product("dvk,vu->dku", z_imag, f_imag)
    v_imag = product("dvk,vu->dku", z_imag, f_real) - product("dvk,vu->dku", z_real, f_imag)
    v_real, v_imag = (v_real * w_real + v_imag * w_imag, v_imag * w_real - v_real * w_imag)
    result = product("tk,dku->dtu", f_real, v_real) + product("tk,dku->dtu", f_imag, v_imag)
    return (result / total_len).reshape(n_series, total_len)


def body(sol_map, resid_map, direction, precond, pixels, angle_index, angles, flag_mask, inv_noise):
    everyone = ("det", "tm")
    share_len = direction.shape[1]
    n_dev = lax.axis_size(everyone)
    copies = jnp.broadcast_to(direction.reshape(1, -1, LANES), (n_dev, direction.size // LANES, LANES))
    gathered = lax.all_to_all(copies, everyone, split_axis=0, concat_axis=0, tiled=True)
    high = n_dev * share_len // LOW
    table = jnp.swapaxes(gathered.reshape(n_dev, 3, share_len), 0, 1).reshape(3 * high, LOW)
    trig = jnp.stack([jnp.cos(2.0 * angles), jnp.sin(2.0 * angles)])
    signal = read_map(trig, table, pixels, angle_index, flag_mask)
    by_detector = lax.all_to_all(signal, "tm", split_axis=0, concat_axis=1, tiled=True)
    filtered = noise_weight(by_detector, inv_noise)
    returned = lax.all_to_all(filtered, "tm", split_axis=1, concat_axis=0, tiled=True)
    partial_map = bin_map(trig, pixels, angle_index, flag_mask, returned, high)
    by_owner = jnp.swapaxes(partial_map.reshape(3, n_dev, share_len), 0, 1)
    image = jnp.sum(lax.all_to_all(by_owner, everyone, split_axis=0, concat_axis=0, tiled=True), axis=0)
    scaled_resid = precond * resid_map
    own_sums = jnp.stack(
        [
            jnp.sum(scaled_resid * resid_map),
            jnp.sum(direction * image),
            jnp.sum(image * scaled_resid),
            jnp.sum(image * precond * image),
        ]
    )
    sum_copies = jnp.broadcast_to(own_sums[None], (n_dev, own_sums.shape[0]))
    all_sums = lax.all_to_all(sum_copies, everyone, split_axis=0, concat_axis=0, tiled=True)
    norm_old, curvature, cross_term, image_norm = jnp.sum(all_sums, axis=0)
    step_size = norm_old / curvature
    new_resid = resid_map - step_size * image
    new_norm = norm_old - 2.0 * step_size * cross_term + step_size * step_size * image_norm
    new_sol = sol_map + step_size * direction
    new_dir = precond * new_resid + new_norm / norm_old * direction
    return (new_sol, new_resid, new_dir, new_norm)


def solution(mesh):
    in_specs = (
        P(None, ("det", "tm")),
        P(None, ("det", "tm")),
        P(None, ("det", "tm")),
        P(None, ("det", "tm")),
        P("det", "tm"),
        P("det", "tm"),
        P(),
        P("det", "tm"),
        P(("det", "tm"), None),
    )
    out_specs = (P(None, ("det", "tm")), P(None, ("det", "tm")), P(None, ("det", "tm")), P())
    return jax.shard_map(body, mesh=mesh, in_specs=in_specs, out_specs=out_specs, check_vma=False)
```

time: 3380 us -> 527 us (0.16)
  other arithmetic: 1670 us -> 7.84 us
  local copies, waits for them, and re-layouts: 1180 us -> 14.8 us
  Pallas kernels: 0 us -> 364 us
  blocking collectives: 347 us -> 61.8 us
  waiting for transfers between devices: 128 us -> 39.3 us
    scatter-add x1 -> x0, other arithmetic: 1400 us -> none  [body(): jnp.zeros((3, n_pixels), jnp.float32).at[:, flat_pix].add(contrib)]
    gather x1 -> x0, local copies, waits for them, and re-layouts: 868 us -> none  [body(): stokes = jnp.take(full_dir, flat_pix, axis=1).reshape(3, det_rows, samples)]
    pallas_call x0 -> x2, Pallas kernels: none -> 364 us  [the longest x1 188 us: read_map(): pl.pallas_call(functools.partial(read_kernel, high=high), out_shape=jax.S...]
    all_gather x1 -> x0, blocking collectives: 276 us -> none  [body(): full_dir = lax.all_gather(direction, ('det', 'tm'), axis=1, tiled=True)]
    slice x2 -> x1, local copies, waits for them, and re-layouts: 186 us -> 1.56 us  [mirrored(): lower = filt[:, :half_len - 1].reshape(n_series, rows, side_len)]
    select_n x2 -> x0, other arithmetic: 134 us -> none  [the longest x1 133 us: body(): stokes = jnp.take(full_dir, flat_pix, axis=1).reshape(3, det_rows, samples)]
    psum x1 -> x0, waiting for transfers between devices: 128 us -> none  [body(): whole = lax.psum(partial_map, ('det', 'tm'))]
    reduce_sum x2 -> x3, other arithmetic: 78.4 us -> 0.82 us  [the longest x1 0.64 us: body(): jnp.sum(scaled_resid * resid_map)]
  transfers between devices with their start and end apart: 2 -> 2, of which waited for: 1 -> 2; matrix products, arithmetic and copies ran while one was open for 1% -> 1% of each run, Pallas kernels for 0% -> 0%
where the time goes in v1:
time: 527 us
  Pallas kernels  364 us (69%)
  blocking collectives  61.8 us (12%)
  waiting for transfers between devices  39.3 us (7%)
  matrix products  21.9 us (4%)
  local copies, waits for them, and re-layouts  14.8 us (3%)
  starting transfers between devices  10.9 us (2%)
  other arithmetic  7.84 us (1%)
  between operations  6.04 us (1%)
    pallas_call x1, Pallas kernels, read_map(): pl.pallas_call(functools.partial(read_kernel, high=high), out_shape=jax.S...  188 us
    pallas_call x1, Pallas kernels, bin_map(): pl.pallas_call(functools.partial(bin_kernel, high=high), out_shape=jax.Sh...  176 us
    all_to_all x1, blocking collectives, body(): lax.all_to_all(filtered, 'tm', split_axis=1, concat_axis=0, tiled=True)  29 us
    all_to_all x1, blocking collectives, body(): lax.all_to_all(by_owner, everyone, split_axis=0, concat_axis=0, tiled=True)  23.6 us
    dot_general x14, matrix products, product(): return jnp.einsum(form, left, right, precision=precision)  21.9 us
    all_to_all x1, waiting for transfers between devices, body(): lax.all_to_all(signal, 'tm', split_axis=0, concat_axis=1, tiled=True)  20.9 us
    all_to_all x1, waiting for transfers between devices, body(): lax.all_to_all(copies, everyone, split_axis=0, concat_axis=0, tiled=True)  18.4 us
  transfers between devices with their start and end apart: 2, of which 2 were waited for; matrix products, arithmetic and copies ran while one was open for 1% of the time, Pallas kernels for 0%

profile of v1, /device:TPU:0, one launch (start us, length us, event | category | flops | bytes accessed | tf_op | source)
XLA Modules:
  0.0 526.6 jit_solution(11339445354091524032)
XLA Ops:
  0.6 0.0 copy-start.4
  0.6 0.8 broadcast_in_dim.6
  1.4 0.9 broadcast_in_dim.7
  2.3 7.3 %all-to-all-start = ((f32[32,36,128]{2,1,0:T(8,128)}), f32[32,36,128]{2,1,0:T(8,128)S(1)}, u32[]{:S(2)}, u32[]{:S(2)}) async-start(f32[32,36,128]{2,1,0:T(8,128)} %broadcast_in_dim.7), calls=%async_computation | async-start | bytes 1310720 | tf_op jit(solution)/shard_map/all_to_all | solution.py:176
  9.6 0.0 copy-done.4
  9.7 0.6 pad_maximum_fusion.1.trig_ref
  10.2 18.4 %all-to-all-done = f32[32,36,128]{2,1,0:T(8,128)S(1)} async-done(((f32[32,36,128]{2,1,0:T(8,128)}), f32[32,36,128]{2,1,0:T(8,128)S(1)}, u32[]{:S(2)}, u32[]{:S(2)}) %all-to-all-start) | async-done | bytes 589856 | tf_op jit(solution)/shard_map/all_to_all | solution.py:176
  28.7 0.2 reshape.69
  28.9 0.2 copy.107
  29.1 1.0 reshape.70.table_ref
  30.0 188.4 %read_map.1 = f32[32,8192]{1,0:T(8,128)} custom-call(f32[2,128]{1,0:T(2,128)} %pad_maximum_fusion.1.trig_ref, f32[576,256]{1,0:T(8,128)} %reshape.70.table_ref, s32[32,8192]{1,0:T(8,128)} %pix_ref.3, s32[32,8192]{1,0:T(8,128)} %ang_ref.3, s32[32,8192]{1,0:T(8,128)} %flag_ref.3), custom_call_target="tpu_custom_call" | custom-call | tf_op jit(solution)/shard_map/read_map/pallas_call | solution.py:104
  218.5 2.6 all_to_all.37
  221.0 3.6 all-to-all-start.1
  224.6 1.6 fusion.102
  226.2 0.5 rev.8
  226.8 0.9 fusion.39
  227.6 0.1 copy.110
  227.8 0.9 sine_negate_fusion
  228.7 0.1 copy.112
  228.8 0.1 copy.171
  228.9 0.7 convolution_bitcast_fusion.3
  229.6 0.6 convolution_bitcast_fusion.2
  230.2 20.9 %all-to-all-done.1 = f32[8,4,8192]{2,1,0:T(4,128)S(1)} async-done(((f32[8,4,8192]{2,1,0:T(4,128)}), f32[8,4,8192]{2,1,0:T(4,128)S(1)}, u32[]{:S(2)}, u32[]{:S(2)}) %all-to-all-start.1) | async-done | bytes 1048608 | tf_op jit(solution)/shard_map/all_to_all | solution.py:181
  251.1 1.6 copy.108
  252.7 1.4 reshape.71
  254.1 1.8 convolution_bitcast_fusion
  255.9 1.8 convolution_bitcast_fusion.1
  257.7 1.7 fusion.23
  259.4 1.7 fusion.37
  261.0 2.0 fusion.3
  263.0 1.7 fusion.5
  264.7 1.6 fusion.34
  266.3 1.6 fusion.32
  267.9 1.6 convolution_add_fusion.1
  269.5 1.6 convolution_subtract_fusion
  271.1 1.6 fusion.9
  272.8 1.9 fusion.1
  274.7 0.3 copy.130
  275.1 0.2 all_to_all.40
  275.3 0.7 copy.131
  276.0 29.0 %all_to_all.51 = f32[4,8,8192]{2,0,1:T(4,128)S(1)} all-to-all(f32[4,8,8192]{2,0,1:T(4,128)S(1)} %copy.131), channel_id=1, replica_groups=mesh['det'=4,'tm'=8] {'tm'}, dimensions={1} | all-to-all | bytes 2097152 | tf_op jit(solution)/shard_map/all_to_all | solution.py:183
  305.0 1.4 all_to_all.43.val_ref
  306.3 175.7 %bin_map.1 = f32[1152,256]{1,0:T(8,128)} custom-call(f32[2,128]{1,0:T(2,128)} %pad_maximum_fusion.1.trig_ref, s32[32,8192]{1,0:T(8,128)} %pix_ref.3, s32[32,8192]{1,0:T(8,128)} %ang_ref.3, s32[32,8192]{1,0:T(8,128)} %flag_ref.3, f32[32,8192]{1,0:T(8,128)} %all_to_all.43.val_ref), custom_call_target="tpu_custom_call" | custom-call | tf_op jit(solution)/shard_map/bin_map/pallas_call | solution.py:120
  482.0 1.3 slice_add_fusion
  483.3 0.2 reshape.74
  483.5 0.4 copy.170
  483.9 0.0 copy-start
  483.9 0.0 copy-start.1
  484.0 0.0 copy-start.2
  484.0 0.0 copy-start.3
  484.0 23.6 %all_to_all.52 = f32[32,3,1536]{2,1,0:T(4,128)S(1)} all-to-all(f32[32,3,1536]{2,1,0:T(4,128)S(1)} %bitcast.91), channel_id=1, replica_groups=mesh['det'=4,'tm'=8] {'det','tm'}, dimensions={0} | all-to-all | bytes 1179648 | tf_op jit(solution)/shard_map/all_to_all | solution.py:186
  507.6 0.1 reduce_sum.55
  507.7 0.0 copy-done
  507.7 0.0 copy-done.1
  507.7 0.0 copy-done.2
  507.7 0.6 multiply_reduce_fusion.2
  508.3 2.7 pad_maximum_fusion.2
  511.0 9.2 %all_to_all.53 = f32[32,1,4]{2,1,0:T(1,128)S(1)} all-to-all(f32[32,1,4]{2,1,0:T(1,128)S(1)} %broadcast_in_dim.8), channel_id=1, replica_groups=mesh['det'=4,'tm'=8] {'det','tm'}, dimensions={0} | all-to-all | bytes 1024 | tf_op jit(solution)/shard_map/all_to_all | solution.py:197
  520.2 0.1 reduce_sum.59
  520.3 0.6 fusion.103
  524.8 0.0 copy-done.3
  524.8 0.6 multiply_add_fusion.3
  (5 shorter events, 0.1 us)
Async XLA Ops:
  0.6 9.0 %copy-start.4 = (f32[128]{0:T(128)S(1)}, f32[128]{0:T(128)}, u32[]{:S(2)}) copy-start(f32[128]{0:T(128)} %param.15) | copy-start | bytes 1540
  2.3 26.4 %all-to-all-start = ((f32[32,36,128]{2,1,0:T(8,128)}), f32[32,36,128]{2,1,0:T(8,128)S(1)}, u32[]{:S(2)}, u32[]{:S(2)}) async-start(f32[32,36,128]{2,1,0:T(8,128)} %broadcast_in_dim.7), calls=%async_computation | async-start | bytes 1310720 | tf_op jit(solution)/shard_map/all_to_all | solution.py:176
  221.0 30.1 %all-to-all-start.1 = ((f32[8,4,8192]{2,1,0:T(4,128)}), f32[8,4,8192]{2,1,0:T(4,128)S(1)}, u32[]{:S(2)}, u32[]{:S(2)}) async-start(f32[8,4,8192]{2,1,0:T(4,128)} %all_to_all.37), calls=%async_computation.1 | async-start | bytes 2097152 | tf_op jit(solution)/shard_map/all_to_all | solution.py:181
  483.9 23.8 %copy-start = (f32[3,1536]{1,0:T(4,128)S(1)}, f32[3,1536]{1,0:T(4,128)}, u32[]{:S(2)}) copy-start(f32[3,1536]{1,0:T(4,128)} %param.11) | copy-start | bytes 55300
  483.9 23.8 %copy-start.1 = (f32[3,1536]{1,0:T(4,128)S(1)}, f32[3,1536]{1,0:T(4,128)}, u32[]{:S(2)}) copy-start(f32[3,1536]{1,0:T(4,128)} %param.12) | copy-start | bytes 55300
  484.0 23.8 %copy-start.2 = (f32[3,1536]{1,0:T(4,128)S(1)}, f32[3,1536]{1,0:T(4,128)}, u32[]{:S(2)}) copy-start(f32[3,1536]{1,0:T(4,128)} %param.10) | copy-start | bytes 55300
  484.0 40.9 %copy-start.3 = (f32[3,1536]{1,0:T(4,128)S(1)}, f32[3,1536]{1,0:T(4,128)}, u32[]{:S(2)}) copy-start(f32[3,1536]{1,0:T(4,128)} %param.9) | copy-start | bytes 55300
